TPU v7x, 1024 devices: a whole 8x8x8 slice. The times are simulated.
1024 devices in a mesh: ep: 16 (over x_lo, y), grp: 64 (over x_hi, z, core).
Axes of the slice: x: 8 (x_hi: 4, x_lo: 2; x = x_hi * 2 + x_lo), y: 8, z: 8, core: 2. Of those that a mesh axis runs over, the one named last changes fastest.
Arguments:
- tokens: bfloat16 [131072, 4096], P(('ep', 'grp')), may hold values from -6 to 6
- expert_ids: int32 [131072, 8], P(('ep', 'grp')), may hold values from 0 to 127, all different within a row; in each aligned block of 128 rows (0 to 127, 128 to 255, ...) at most 16 rows name the same one
- combine: float32 [131072, 8], P(('ep', 'grp')), may hold values from 0.05 to 1
- w_gate: bfloat16 [4096, 5120], P(None, 'ep'), may hold values from -0.09375 to 0.09375
- w_up: bfloat16 [4096, 5120], P(None, 'ep'), may hold values from -0.09375 to 0.09375
- w_down: bfloat16 [5120, 4096], P('ep'), may hold values from -0.15625 to 0.15625
- bias: float32 [128], replicated, may hold values from -3 to 3
Outputs:
- mixed: bfloat16 [131072, 4096], P(('ep', 'grp'))
- new_bias: float32 [128], replicated
Inputs may be any that keep to these rules, and one draw needn't show every extreme that they name: `expert_ids`: each row names 8 different experts. Among the rows of one device no expert is named more than 16 times, a bound that some block reaches.
All inputs are finite; a program needn't handle non-finite values.
Results may differ from a plain program's by a relative error of at most 0.0057.
Values may be sent and summed in bfloat16 or wider, within the bound.
A program may use at most 32 MiB of HBM per device.

v0:
```python
import jax
import jax.numpy as jnp
from jax import lax
from jax.sharding import Mesh
from jax.sharding import PartitionSpec as P

NEXP = 128
TOPK = 8
SPLIT = 4
GRP = ("grp_0", "grp_1", "grp_2")
EP_GRP = ("ep", "grp_0", "grp_1", "grp_2")


def sent_to_all(value, axis):
    devices = lax.axis_size(axis)
    return lax.all_to_all(
        jnp.broadcast_to(value[None], (devices, *value.shape)), axis, 0, 0, tiled=True
    )


def taken_together(value, axis):
    return sent_to_all(value, axis).sum(axis=0)


def by_axis(value, axes):
    for axis in axes:
        value = lax.psum(value, axis)
    return value


def count_loads(expert_ids):
    experts = jnp.arange(NEXP, dtype=jnp.int32)
    local = jnp.sum(
        (expert_ids.reshape(-1)[:, None] == experts[None, :]).astype(jnp.float32), axis=0
    )
    within = taken_together(local, "ep")
    return by_axis(within, GRP)


def per_device(tokens, expert_ids, combine, w_gate, w_up, w_down, bias):
    n_ep = lax.axis_size("ep")
    n_grp = lax.axis_size(GRP)
    tok_rows = tokens.shape[0]
    width = tokens.shape[1]
    capacity = tok_rows // 8
    win_experts = n_ep // SPLIT
    flat_ids = expert_ids.reshape(-1)
    window = jnp.arange(win_experts, dtype=jnp.int32)
    hit = (flat_ids[:, None] == window[None, :]).astype(jnp.int32)
    ranks = jnp.cumsum(hit, axis=0) - 1
    slot = jnp.sum(hit * ranks, axis=1)
    inside = jnp.sum(hit, axis=1)
    dest = jnp.where(inside > 0, flat_ids * capacity + slot, win_experts * capacity)
    slot_ids = jnp.arange(win_experts * capacity, dtype=jnp.int32)
    chosen = (slot_ids[:, None] == dest[None, :]).reshape(win_experts * capacity, tok_rows, TOPK)
    select = jnp.sum(chosen.astype(jnp.float32), axis=2)
    weights = jnp.sum(chosen.astype(jnp.float32) * combine[None, :, :], axis=2)
    buffer = jnp.dot(
        select.astype(jnp.bfloat16), tokens, preferred_element_type=jnp.float32
    ).astype(jnp.bfloat16)
    outgoing = jnp.repeat(buffer.reshape(win_experts, capacity, width), SPLIT, axis=0)
    block = lax.all_to_all(outgoing, "ep", split_axis=0, concat_axis=0, tiled=True)
    rows = block.reshape(-1, width)
    gate = jnp.dot(rows, w_gate, preferred_element_type=jnp.float32)
    upval = jnp.dot(rows, w_up, preferred_element_type=jnp.float32)
    hidden = (jax.nn.silu(gate) * upval).astype(jnp.bfloat16)
    part = jnp.dot(hidden, w_down, preferred_element_type=jnp.float32).astype(jnp.bfloat16)
    returned = lax.all_to_all(
        part.reshape(block.shape), "ep", split_axis=0, concat_axis=0, tiled=True
    )
    summed = jnp.sum(
        returned.astype(jnp.float32).reshape(win_experts, SPLIT, capacity, width), axis=1
    )
    summed = summed.reshape(win_experts * capacity, width)
    mixed = jnp.dot(
        weights.T, summed, precision=lax.Precision.HIGHEST, preferred_element_type=jnp.float32
    ).astype(jnp.bfloat16)
    load = count_loads(expert_ids)
    mean_load = jnp.float32(tok_rows * n_ep * n_grp * TOPK / NEXP)
    new_bias = bias - 0.05 * (load - mean_load) / jnp.sqrt(mean_load)
    return (mixed, new_bias)


def solution(mesh):
    finer = Mesh(mesh.devices.reshape(mesh.shape["ep"], 4, 8, 2), ("ep", "grp_0", "grp_1", "grp_2"))
    in_specs = (
        P(EP_GRP, None),
        P(EP_GRP, None),
        P(EP_GRP, None),
        P(None, "ep"),
        P(None, "ep"),
        P("ep", None),
        P(),
    )
    out_specs = (P(EP_GRP, None), P())
    return jax.shard_map(
        per_device, mesh=finer, in_specs=in_specs, out_specs=out_specs, check_vma=False
    )
```

profile of v0, /device:TPU:1, one launch (start us, length us, event | category | flops | bytes accessed | tf_op | source)
XLA Modules:
  0.0 175.1 jit_solution(15120958893424985419)
XLA Ops:
  0.6 0.0 copy-start
  0.6 0.9 copy.27
  1.6 0.1 eq.53
  1.7 0.1 eq.57
  1.8 1.1 reduce-window.6
  2.9 0.2 slice_reduce_fusion
  3.1 0.2 reduce-window.9
  3.3 0.1 add_bitcast_fusion
  3.5 0.1 gt.15
  3.6 0.1 copy.30
  3.6 0.1 reduce_sum.67
  3.8 0.7 add_select_fusion
  4.5 0.8 convert_reduce_fusion.2
  5.3 1.5 convolution_convert_fusion.2
  6.9 1.5 broadcast_in_dim.9
  8.4 9.2 %all-to-all-start = ((bf16[16,16,4096]{2,1,0:T(8,128)(2,1)}), bf16[16,16,4096]{2,1,0:T(8,128)(2,1)}, u32[]{:S(2)}, u32[]{:S(2)}) async-start(bf16[16,16,4096]{2,1,0:T(8,128)(2,1)} %bitcast.33), calls=%async_computation | async-start | bytes 4194304 | tf_op jit(solution)/shard_map/all_to_all | solution.py:62
  17.6 0.2 convert_reduce_fusion.1
  17.8 51.8 %all-to-all-done = bf16[16,16,4096]{2,1,0:T(8,128)(2,1)} async-done(((bf16[16,16,4096]{2,1,0:T(8,128)(2,1)}), bf16[16,16,4096]{2,1,0:T(8,128)(2,1)}, u32[]{:S(2)}, u32[]{:S(2)}) %all-to-all-start) | async-done | bytes 2097184 | tf_op jit(solution)/shard_map/all_to_all | solution.py:62
  69.6 0.6 broadcast_in_dim.10
  70.2 5.7 %all-to-all-start.2 = ((f32[16,1,128]{2,1,0:T(1,128)}), f32[16,1,128]{2,1,0:T(1,128)S(1)}, u32[]{:S(2)}, u32[]{:S(2)}) async-start(f32[16,1,128]{2,1,0:T(1,128)} %broadcast_in_dim.10), calls=%async_computation.2 | async-start | bytes 16384 | tf_op jit(solution)/shard_map/all_to_all | solution.py:16
  75.8 3.2 %fusion.12 = f32[256,320]{0,1:T(8,128)S(1)} fusion(bf16[256,4096]{1,0:T(8,128)(2,1)} %bitcast.3, bf16[4096,320]{0,1:T(8,128)(2,1)} %param.10), kind=kOutput, calls=%fused_computation.31 | convolution fusion | flops 671088640 | bytes 5046272 | tf_op jit(solution)/shard_map/dot_general | solution.py:64
  79.1 0.0 copy-done
  79.1 7.2 %convolution_convert_fusion = bf16[256,4096]{1,0:T(8,128)(2,1)} fusion(bf16[320,4096]{1,0:T(8,128)(2,1)S(1)} %copy-done, bf16[256,4096]{1,0:T(8,128)(2,1)} %bitcast.3, bf16[4096,320]{0,1:T(8,128)(2,1)} %param.11, f32[256,320]{0,1:T(8,128)S(1)} %fusion.12), kind=kOutput, calls=%fused_computation | convolution fusion | flops 1343717376 | bytes 9764864 | tf_op jit(solution)/shard_map/dot_general | solution.py:67
  86.3 0.0 all-to-all-done.2
  86.3 7.7 %all-to-all-start.1 = ((bf16[16,16,4096]{2,1,0:T(8,128)(2,1)}), bf16[16,16,4096]{2,1,0:T(8,128)(2,1)}, u32[]{:S(2)}, u32[]{:S(2)}) async-start(bf16[16,16,4096]{2,1,0:T(8,128)(2,1)} %bitcast.36), calls=%async_computation.1 | async-start | bytes 4194304 | tf_op jit(solution)/shard_map/all_to_all | solution.py:68
  94.0 38.9 %psum.21 = f32[128]{0:T(128)S(1)} all-reduce(f32[128]{0:T(128)S(1)} %reduce_sum.72), channel_id=1, replica_groups=mesh['ep'=16,'grp_0'=4,'grp_1'=8,'grp_2'=2] {'grp_0'}, use_global_device_ids=true, to_apply=%region_9.10 | all-reduce | flops 128 | bytes 1024 | tf_op jit(solution)/shard_map/psum | solution.py:27
  132.9 26.5 %psum.22 = f32[128]{0:T(128)S(1)} all-reduce(f32[128]{0:T(128)S(1)} %psum.21), channel_id=1, replica_groups=mesh['ep'=16,'grp_0'=4,'grp_1'=8,'grp_2'=2] {'grp_1'}, use_global_device_ids=true, to_apply=%region_10.11 | all-reduce | flops 128 | bytes 1024 | tf_op jit(solution)/shard_map/psum | solution.py:27
  159.5 10.2 %psum.23 = f32[128]{0:T(128)S(1)} all-reduce(f32[128]{0:T(128)S(1)} %psum.22), channel_id=1, replica_groups=mesh['ep'=16,'grp_0'=4,'grp_1'=8,'grp_2'=2] {'grp_2'}, use_global_device_ids=true, to_apply=%region_11.12 | all-reduce | flops 128 | bytes 1024 | tf_op jit(solution)/shard_map/psum | solution.py:27
  169.7 0.5 multiply_subtract_fusion
  170.2 0.0 all-to-all-done.1
  170.2 2.1 %convert_reduce_fusion = f32[4,16,4096]{2,1,0:T(8,128)S(1)} fusion(bf16[16,16,4096]{2,1,0:T(8,128)(2,1)} %all-to-all-done.1), kind=kLoop, calls=%fused_computation.3 | loop fusion | flops 1835008 | bytes 3145728 | tf_op jit(solution)/shard_map/reduce_sum | solution.py:71
  172.3 2.8 %convolution_convert_fusion.1 = bf16[128,4096]{1,0:T(8,128)(2,1)} fusion(f32[64,128]{1,0:T(8,128)S(1)} %get-tuple-element.3, f32[64,4096]{1,0:T(8,128)S(1)} %bitcast.34), kind=kOutput, calls=%fused_computation.1 | convolution fusion | flops 403177472 | bytes 2129920 | tf_op jit(solution)/shard_map/dot_general | solution.py:75
  (7 shorter events, 0.1 us)
Async XLA Ops:
  0.6 78.5 %copy-start = (bf16[320,4096]{1,0:T(8,128)(2,1)S(1)}, bf16[320,4096]{1,0:T(8,128)(2,1)}, u32[]{:S(2)}) copy-start(bf16[320,4096]{1,0:T(8,128)(2,1)} %param.12) | copy-start | bytes 7864324
  8.4 61.2 %all-to-all-start = ((bf16[16,16,4096]{2,1,0:T(8,128)(2,1)}), bf16[16,16,4096]{2,1,0:T(8,128)(2,1)}, u32[]{:S(2)}, u32[]{:S(2)}) async-start(bf16[16,16,4096]{2,1,0:T(8,128)(2,1)} %bitcast.33), calls=%async_computation | async-start | bytes 4194304 | tf_op jit(solution)/shard_map/all_to_all | solution.py:62
  70.2 16.1 %all-to-all-start.2 = ((f32[16,1,128]{2,1,0:T(1,128)}), f32[16,1,128]{2,1,0:T(1,128)S(1)}, u32[]{:S(2)}, u32[]{:S(2)}) async-start(f32[16,1,128]{2,1,0:T(1,128)} %broadcast_in_dim.10), calls=%async_computation.2 | async-start | bytes 16384 | tf_op jit(solution)/shard_map/all_to_all | solution.py:16
  86.3 83.5 %copy-start.1 = (f32[128]{0:T(128)S(1)}, f32[128]{0:T(128)}, u32[]{:S(2)}) copy-start(f32[128]{0:T(128)} %param.13) | copy-start | bytes 1540
  86.3 84.0 %all-to-all-start.1 = ((bf16[16,16,4096]{2,1,0:T(8,128)(2,1)}), bf16[16,16,4096]{2,1,0:T(8,128)(2,1)}, u32[]{:S(2)}, u32[]{:S(2)}) async-start(bf16[16,16,4096]{2,1,0:T(8,128)(2,1)} %bitcast.36), calls=%async_computation.1 | async-start | bytes 4194304 | tf_op jit(solution)/shard_map/all_to_all | solution.py:68
where the time goes:
time: 176 us; the launch traced here: 175 us
  blocking collectives  75.7 us (43%)
  waiting for transfers between devices  51.8 us (29%)
  starting transfers between devices  22.6 us (13%)
  matrix products  14.7 us (8%)
  other arithmetic  5.81 us (3%)
  local copies, waits for them, and re-layouts  3.8 us (2%)
    psum x3, blocking collectives, by_axis(): value = lax.psum(value, axis)  75.7 us
    all_to_all x1, waiting for transfers between devices, per_device(): lax.all_to_all(outgoing, 'ep', split_axis=0, concat_axis=0, tiled=True)  51.8 us
    all_to_all x1, starting transfers between devices, per_device(): lax.all_to_all(outgoing, 'ep', split_axis=0, concat_axis=0, tiled=True)  9.17 us
    all_to_all x1, starting transfers between devices, per_device(): lax.all_to_all(part.reshape(block.shape), 'ep', split_axis=0, concat_axis...  7.74 us
    dot_general x1, matrix products, per_device(): jnp.dot(hidden, w_down, preferred_element_type=jnp.float32)  7.15 us
    all_to_all x1, starting transfers between devices, sent_to_all(): lax.all_to_all(jnp.broadcast_to(value[None], (devices, *value.shape)), ax...  5.66 us
  transfers between devices with their start and end apart: 3, of which 1 were waited for; matrix products, arithmetic and copies ran while one was open for 6% of the time, Pallas kernels for 0%

commit v1 on v0

v1 whole, which is shorter than its diff:
```python
import functools
import math

import jax
import jax.numpy as jnp
from jax import lax
from jax.experimental import pallas as pl
from jax.experimental.pallas import tpu as pltpu
from jax.sharding import Mesh
from jax.sharding import PartitionSpec as P

NEXP = 128
TOPK = 8
NWIN = 4
CAP = 16
AXES = ("xl", "y", "xh", "z", "c")
MESH = pl.DeviceIdType.MESH
f32 = jnp.float32
bf16 = jnp.bfloat16


def kernel(
    sizes, mean_load,
    ids_ref, comb_ref, bias_ref, tok_hbm, wg_hbm, wu_hbm, wd_hbm,
    mixed_ref, nb_ref,
    tok, wg, wu, wd, ent, xbuf, part, ret, fin, sw, lsend, lrecv,
    in_sem, ent_ss, fr_ss, fl_ss, x_rs, rr_ss, rl_ss, r_rs, fx_ss, f_rs, l_ss, l_rs,
):
    nxh, nz, nc = sizes
    width = tok.shape[1]
    xl, y = lax.axis_index("xl"), lax.axis_index("y")
    xh, z, c = lax.axis_index("xh"), lax.axis_index("z"), lax.axis_index("c")
    quad, s = lax.div(y, 4), lax.rem(y, 4)
    own = 2 * xl + quad
    mate = 1 - xl

    loads = [
        pltpu.make_async_copy(tok_hbm, tok, in_sem.at[0]),
        pltpu.make_async_copy(wg_hbm, wg, in_sem.at[1]),
        pltpu.make_async_copy(wu_hbm, wu, in_sem.at[2]),
        pltpu.make_async_copy(wd_hbm, wd, in_sem.at[3]),
    ]
    for copy in loads:
        copy.start()

    nx = 2 * nxh
    xi = 2 * xh + xl
    y_peers = [(lax.rem(y + k, 8), {"y": lax.rem(y + k, 8)}) for k in range(1, 8)]
    x_peers = []
    for k in range(1, nx):
        other = lax.rem(xi + k, nx)
        x_peers.append((other, {"xl": lax.rem(other, 2), "xh": lax.div(other, 2)}))
    z_peers = [(lax.rem(z + k, nz), {"z": lax.rem(z + k, nz)}) for k in range(1, nz)]
    c_peers = [(lax.rem(c + k, nc), {"c": lax.rem(c + k, nc)}) for k in range(1, nc)]
    greeted = [where for _, where in y_peers + x_peers + z_peers + c_peers]
    for dy in (-2, -1, 1, 2):
        greeted.append({"xl": mate, "y": lax.rem(y + dy + 8, 8)})
    barrier = pltpu.get_barrier_semaphore()
    for where in greeted:
        pl.semaphore_signal(barrier, inc=1, device_id=where, device_id_type=MESH)

    ids = ids_ref[...]
    comb = comb_ref[...]
    row8 = lax.broadcasted_iota(jnp.int32, (8, 128), 0)
    exps = lax.broadcasted_iota(jnp.int32, (NEXP, 128), 0)
    hit = jnp.zeros((8, 128), f32)
    weight = jnp.zeros((8, 128), f32)
    many = jnp.zeros((NEXP, 128), f32)
    for p in range(TOPK):
        named = ids[p : p + 1, :]
        same = row8 == named
        hit += jnp.where(same, 1.0, 0.0)
        weight += jnp.where(same, comb[p : p + 1, :], 0.0)
        many += jnp.where(exps == named, 1.0, 0.0)
    before = lax.broadcasted_iota(jnp.int32, (128, 128), 0) < lax.broadcasted_iota(
        jnp.int32, (128, 128), 1
    )
    rank = jnp.dot(
        hit.astype(bf16), jnp.where(before, 1.0, 0.0).astype(bf16), preferred_element_type=f32
    )
    slots = lax.broadcasted_iota(jnp.int32, (CAP, 128), 0).astype(f32)
    select, scale = [], []
    for w in range(NWIN):
        there = jnp.where(slots == rank[w : w + 1, :], hit[w : w + 1, :], 0.0)
        select.append(there)
        scale.append(there * weight[w : w + 1, :])
    select = jnp.concatenate(select, axis=0).astype(bf16)
    scale = jnp.concatenate(scale, axis=0)
    high = scale.astype(bf16)
    rest = scale - high.astype(f32)
    middle = rest.astype(bf16)
    low = (rest - middle.astype(f32)).astype(bf16)
    sw[...] = jnp.concatenate([high, middle, low], axis=0)
    counts = lax.dot_general(
        jnp.ones((8, 128), bf16), many.astype(bf16), (((1,), (1,)), ((), ())),
        preferred_element_type=f32,
    )
    lsend[0] = counts

    loads[0].wait()
    step = min(1024, width)
    for at in range(0, width, step):
        rows = jnp.dot(select, tok[:, at : at + step], preferred_element_type=f32)
        ent[:, at : at + step] = rows.astype(bf16)
    xbuf[s + 2, 0:CAP, :] = ent[pl.ds(pl.multiple_of(own * CAP, CAP), CAP), :]

    pl.semaphore_wait(barrier, len(greeted))

    entries = []
    for number, (k, dx) in enumerate(((0, 1), (1, 0), (1, 1))):
        tq = lax.rem(quad + k, 2)
        tx = lax.rem(xl + dx, 2)
        ry = lax.rem(y - 4 * tq + 8, 8)
        o = jnp.where(ry <= 5, ry, ry - 8)
        node = jnp.clip(o, 0, 3)
        w = 2 * tx + tq
        entries.append(
            pltpu.make_async_remote_copy(
                src_ref=ent.at[pl.ds(pl.multiple_of(w * CAP, CAP), CAP)],
                dst_ref=xbuf.at[o + 2, pl.ds(CAP * dx, CAP)],
                send_sem=ent_ss.at[number],
                recv_sem=x_rs.at[o + 2, dx],
                device_id={"xl": tx, "y": 4 * tq + node},
                device_id_type=MESH,
            )
        )

    def forward(i, xr, right):
        block = xbuf.at[i, pl.ds(CAP * xr, CAP)]
        return pltpu.make_async_remote_copy(
            src_ref=block,
            dst_ref=block,
            send_sem=(fr_ss if right else fl_ss).at[i, xr],
            recv_sem=x_rs.at[i, xr],
            device_id={"y": lax.rem(y + (1 if right else 7), 8)},
            device_id_type=MESH,
        )

    entries[0].start()

    @pl.when(s < 3)
    def _():
        forward(s + 2, 0, True).start()

    @pl.when(s > 0)
    def _():
        forward(s + 2, 0, False).start()

    entries[1].start()
    entries[2].start()

    def tell(phase, number, here, peers):
        made = []
        for k, (_, where) in enumerate(peers):
            made.append(
                pltpu.make_async_remote_copy(
                    src_ref=lsend.at[phase],
                    dst_ref=lrecv.at[phase, here],
                    send_sem=l_ss.at[phase, k],
                    recv_sem=l_rs.at[phase, here],
                    device_id=where,
                    device_id_type=MESH,
                )
            )
        return made

    phases = [(y, y_peers), (xi, x_peers), (z, z_peers), (c, c_peers)]

    def tell_all(phase):
        for copy in tell(phase, None, phases[phase][0], phases[phase][1]):
            copy.start()

    def hear_all(phase):
        total = lsend[phase]
        for other, where in phases[phase][1]:
            pltpu.make_async_remote_copy(
                src_ref=lsend.at[phase],
                dst_ref=lrecv.at[phase, other],
                send_sem=l_ss.at[phase, 0],
                recv_sem=l_rs.at[phase, other],
                device_id=where,
                device_id_type=MESH,
            ).wait_recv()
            total = total + lrecv[phase, other]
        return total

    tell_all(0)
    for copy in loads[1:]:
        copy.wait()

    def send_back(i, xr, right):
        block = ret.at[i, pl.ds(CAP * xr, CAP)]
        o = i - 2
        to = lax.rem(y + (1 if right else 7), 8)
        slot = i if right else jnp.where(o == s - 1, 8, i)
        inner = pltpu.make_async_remote_copy(
            src_ref=block,
            dst_ref=ret.at[slot, pl.ds(CAP * xr, CAP)],
            send_sem=(rr_ss if right else rl_ss).at[i, xr],
            recv_sem=r_rs.at[slot, xr],
            device_id={"y": to},
            device_id_type=MESH,
        )
        outer = pltpu.make_async_remote_copy(
            src_ref=block,
            dst_ref=fin.at[own],
            send_sem=(rr_ss if right else rl_ss).at[i, xr],
            recv_sem=f_rs.at[own],
            device_id={
                "xl": lax.rem(xl + xr, 2),
                "y": lax.rem(4 * quad + o + 8, 8),
            },
            device_id_type=MESH,
        )
        return inner, outer

    def arrived(i, xr):
        block = ret.at[i, pl.ds(CAP * xr, CAP)]
        pltpu.make_async_remote_copy(
            src_ref=block, dst_ref=block, send_sem=rr_ss.at[0, xr], recv_sem=r_rs.at[i, xr],
            device_id={"y": lax.rem(y + 1, 8)}, device_id_type=MESH,
        ).wait_recv()

    def to_mate():
        return pltpu.make_async_remote_copy(
            src_ref=ret.at[9, pl.ds(0, CAP)],
            dst_ref=fin.at[own],
            send_sem=fx_ss.at[0],
            recv_sem=f_rs.at[own],
            device_id={"xl": mate},
            device_id_type=MESH,
        )

    last = jnp.maximum(2 * s, 6 - 2 * s)

    def round_(r, carry):
        ol, orr = s - r, s + r
        has_l = (r >= 1) & (ol >= -2)
        has_r = (r >= 1) & (orr <= 5)
        il = jnp.where(has_l, ol, s) + 2
        ir = jnp.where(has_r, orr, s) + 2

        @pl.when(r == 0)
        def _():
            forward(s + 2, 1, True).wait_recv()

            @pl.when(s < 3)
            def _():
                forward(s + 2, 1, True).start()

            @pl.when(s > 0)
            def _():
                forward(s + 2, 1, False).start()

        for xr in (0, 1):

            @pl.when(has_l)
            def _():
                forward(il, xr, True).wait_recv()

                @pl.when(s < 3)
                def _():
                    forward(il, xr, True).start()

            @pl.when(has_r)
            def _():
                forward(ir, xr, False).wait_recv()

                @pl.when(s > 0)
                def _():
                    forward(ir, xr, False).start()

        for phase in range(3):

            @pl.when(r == phase + 1)
            def _():
                lsend[phase + 1] = hear_all(phase)
                tell_all(phase + 1)

        @pl.when(r == 4)
        def _():
            load = hear_all(3)[0:1, :]
            nb_ref[...] = bias_ref[...] - 0.05 * (load - mean_load) / math.sqrt(mean_load)

        @pl.when((r == 0) | has_l | has_r)
        def _():
            rows = jnp.concatenate([xbuf[il], xbuf[ir]], axis=0)
            flat = (((1,), (1,)), ((), ()))
            gate = lax.dot_general(wg[...], rows, flat, preferred_element_type=f32)
            up = lax.dot_general(wu[...], rows, flat, preferred_element_type=f32)
            hidden = (jax.nn.silu(gate) * up).astype(bf16)
            for at in range(0, width, step):
                out = lax.dot_general(
                    hidden, wd[:, at : at + step], (((0,), (0,)), ((), ())),
                    preferred_element_type=f32,
                )
                part[il, :, at : at + step] = out[: 2 * CAP]
                part[ir, :, at : at + step] = out[2 * CAP :]

        for right in (True, False):
            o = r - s if right else 6 - s - r
            valid = (o > s) & (o <= 5) if right else (o < s) & (o >= -2)
            i = o + 2
            first = s == (0 if right else 3)
            end = s == (3 if right else 0)

            for xr in (0, 1):
                span = pl.ds(CAP * xr, CAP)

                @pl.when(valid)
                def _():
                    @pl.when(first)
                    def _():
                        ret[i, span, :] = part[i, span, :].astype(bf16)

                    @pl.when(jnp.logical_not(first))
                    def _():
                        arrived(i, xr)
                        ret[i, span, :] = (part[i, span, :] + ret[i, span, :].astype(f32)).astype(
                            bf16
                        )

                    inner, outer = send_back(i, xr, right)

                    @pl.when(end)
                    def _():
                        outer.start()

                    @pl.when(jnp.logical_not(end))
                    def _():
                        inner.start()

        @pl.when(r == last)
        def _():
            for xr in (1, 0):
                span = pl.ds(CAP * xr, CAP)

                @pl.when(s > 0)
                def _():
                    arrived(s + 2, xr)
                    part[s + 2, span, :] += ret[s + 2, span, :].astype(f32)

                @pl.when(s < 3)
                def _():
                    arrived(8, xr)
                    part[s + 2, span, :] += ret[8, span, :].astype(f32)

                if xr == 1:
                    ret[9, 0:CAP, :] = part[s + 2, span, :].astype(bf16)
                    to_mate().start()
                else:
                    fin[own] = part[s + 2, span, :].astype(bf16)

        return carry

    lax.fori_loop(0, 9, round_, 0)

    for k, dx in ((0, 1), (1, 0), (1, 1)):
        w = 2 * lax.rem(xl + dx, 2) + lax.rem(quad + k, 2)
        pltpu.make_async_remote_copy(
            src_ref=ret.at[9, pl.ds(0, CAP)], dst_ref=fin.at[w], send_sem=fx_ss.at[0],
            recv_sem=f_rs.at[w], device_id={"xl": mate}, device_id_type=MESH,
        ).wait_recv()
    wide = min(512, width)
    for at in range(0, width, wide):
        done = fin[:, :, at : at + wide].reshape(NWIN * CAP, wide)
        done = jnp.concatenate([done, done, done], axis=0)
        mixed_ref[:, at : at + wide] = lax.dot_general(
            sw[...], done, (((0,), (0,)), ((), ())), preferred_element_type=f32
        ).astype(bf16)

    for copy in entries:
        copy.wait_send()
    to_mate().wait_send()
    for phase in range(4):
        for copy in tell(phase, None, phases[phase][0], phases[phase][1]):
            copy.wait_send()

    def drain(i, carry):
        o = i - 2
        for xr in (0, 1):

            @pl.when((s < 3) & (o <= s))
            def _():
                forward(i, xr, True).wait_send()

            @pl.when((s > 0) & (o >= s))
            def _():
                forward(i, xr, False).wait_send()

            @pl.when(o > s)
            def _():
                send_back(i, xr, True)[1].wait_send()

            @pl.when(o < s)
            def _():
                send_back(i, xr, False)[1].wait_send()

        return carry

    lax.fori_loop(0, 8, drain, 0)


def per_device(sizes, tokens, expert_ids, combine, w_gate, w_up, w_down, bias):
    tok_rows, width = tokens.shape
    hidden = w_down.shape[0]
    devices = 16 * math.prod(sizes)
    mean_load = float(tok_rows * devices * TOPK / NEXP)
    vmem = pl.BlockSpec(memory_space=pltpu.VMEM)
    hbm = pl.BlockSpec(memory_space=pl.ANY)
    dma = pltpu.SemaphoreType.DMA
    mixed, new_bias = pl.pallas_call(
        functools.partial(kernel, sizes, mean_load),
        out_shape=(
            jax.ShapeDtypeStruct((tok_rows, width), bf16),
            jax.ShapeDtypeStruct((1, NEXP), f32),
        ),
        in_specs=[vmem, vmem, vmem, hbm, hbm, hbm, hbm],
        out_specs=(vmem, vmem),
        scratch_shapes=[
            pltpu.VMEM((tok_rows, width), bf16),
            pltpu.VMEM((hidden, width), bf16),
            pltpu.VMEM((hidden, width), bf16),
            pltpu.VMEM((hidden, width), bf16),
            pltpu.VMEM((NWIN * CAP, width), bf16),
            pltpu.VMEM((8, 2 * CAP, width), bf16),
            pltpu.VMEM((8, 2 * CAP, width), f32),
            pltpu.VMEM((10, 2 * CAP, width), bf16),
            pltpu.VMEM((NWIN, CAP, width), bf16),
            pltpu.VMEM((3 * NWIN * CAP, 128), bf16),
            pltpu.VMEM((4, 8, 128), f32),
            pltpu.VMEM((4, 8, 8, 128), f32),
            dma((4,)),
            dma((3,)),
            dma((8, 2)),
            dma((8, 2)),
            dma((8, 2)),
            dma((8, 2)),
            dma((8, 2)),
            dma((10, 2)),
            dma((1,)),
            dma((NWIN,)),
            dma((4, 8)),
            dma((4, 8)),
        ],
        compiler_params=pltpu.CompilerParams(
            collective_id=0, has_side_effects=True, vmem_limit_bytes=48 * 1024 * 1024
        ),
        name="moe",
    )(
        expert_ids.T, combine.T, bias.reshape(1, NEXP), tokens, w_gate.T, w_up.T, w_down,
    )
    return mixed, new_bias.reshape(NEXP)


def solution(mesh):
    devices = mesh.devices
    ep, grp = devices.shape
    shape = (2, 8, 4, 8, 2) if (ep, grp) == (16, 64) else (2, 8, 1, 1, grp)
    finer = Mesh(devices.reshape(shape), AXES)
    row = P(AXES, None)
    in_specs = (row, row, row, P(None, ("xl", "y")), P(None, ("xl", "y")), P(("xl", "y"), None), P())
    return jax.shard_map(
        functools.partial(per_device, shape[2:]), mesh=finer, in_specs=in_specs,
        out_specs=(row, P()), check_vma=False,
    )
```

time: 176 us -> 100 us (0.57)
  the two profiles are of different devices: /device:TPU:1 before, /device:TPU:36 now
where the time goes in v1:
time: 100 us
  Pallas kernels  93 us (93%)
  local copies, waits for them, and re-layouts  6.47 us (6%)
    pallas_call x1, Pallas kernels, per_device(): pl.pallas_call(functools.partial(kernel, sizes, mean_load), out_shape=(ja...  93 us
    unnamed x12, local copies, waits for them, and re-layouts  6.47 us

profile of v1, /device:TPU:36, one launch (start us, length us, event | category | flops | bytes accessed | tf_op | source)
XLA Modules:
  0.0 100.1 jit_solution(3139701385703927335)
XLA Ops:
  0.6 0.0 copy-start
  0.6 1.7 %copy-done = bf16[4096,320]{0,1:T(8,128)(2,1)S(1)} copy-done((bf16[4096,320]{0,1:T(8,128)(2,1)S(1)}, bf16[4096,320]{0,1:T(8,128)(2,1)}, u32[]{:S(2)}) %copy-start) | copy-done | bytes 2621464
  2.4 0.0 copy-start.1
  2.4 1.2 %copy-done.1 = bf16[128,4096]{1,0:T(8,128)(2,1)S(1)} copy-done((bf16[128,4096]{1,0:T(8,128)(2,1)S(1)}, bf16[128,4096]{1,0:T(8,128)(2,1)}, u32[]{:S(2)}) %copy-start.1) | copy-done | bytes 1048600
  3.6 0.0 copy-start.2
  3.6 0.7 copy-done.2
  4.3 0.0 copy-start.3
  4.3 0.7 copy-done.3
  5.0 0.0 copy-start.4
  5.0 0.7 copy-done.4
  5.6 93.0 %moe.1 = (bf16[128,4096]{1,0:T(8,128)(2,1)S(1)}, f32[1,128]{1,0:T(1,128)S(1)}) custom-call(s32[8,128]{1,0:T(8,128)S(1)} %bitcast.7, f32[8,128]{1,0:T(8,128)S(1)} %bitcast.8, f32[1,128]{1,0:T(1,128)S(1)} %bitcast.9, bf16[128,4096]{1,0:T(8,128)(2,1)S(1)} %copy-done.1, bf16[320,4096]{1,0:T(8,128)(2,1)S(1)} %bitcast.6, bf16[320,4096]{1,0:T(8,128)(2,1)} %bitcast.11, ...), custom_call_target="tpu_custom_call" | custom-call | tf_op jit(solution)/shard_map/moe/pallas_call | solution.py:412
  98.6 1.0 copy.11
  99.6 0.5 copy.12
Async XLA Ops:
  0.6 1.7 %copy-start = (bf16[4096,320]{0,1:T(8,128)(2,1)S(1)}, bf16[4096,320]{0,1:T(8,128)(2,1)}, u32[]{:S(2)}) copy-start(bf16[4096,320]{0,1:T(8,128)(2,1)} %param.10) | copy-start | bytes 7864324
  2.4 1.2 %copy-start.1 = (bf16[128,4096]{1,0:T(8,128)(2,1)S(1)}, bf16[128,4096]{1,0:T(8,128)(2,1)}, u32[]{:S(2)}) copy-start(bf16[128,4096]{1,0:T(8,128)(2,1)} %tok_hbm.1) | copy-start | bytes 3145732
  3.6 0.7 copy-start.2
  4.3 0.7 copy-start.3
  5.0 0.7 copy-start.4

commit v2 on v1

v2 whole, which is shorter than its diff:
```python
import functools
import math

import jax
import jax.numpy as jnp
from jax import lax
from jax.experimental import pallas as pl
from jax.experimental.pallas import tpu as pltpu
from jax.sharding import Mesh
from jax.sharding import PartitionSpec as P

NEXP = 128
TOPK = 8
NWIN = 4
CAP = 16
PIECES = 4
AXES = ("xl", "y", "xh", "z", "c")
MESH = pl.DeviceIdType.MESH
f32 = jnp.float32
bf16 = jnp.bfloat16


def kernel(
    sizes, mean_load,
    ids_hbm, comb_hbm, bias_hbm, tok_hbm, wg_hbm, wu_hbm, wd_hbm,
    mixed_ref, nb_ref,
    ids_ref, comb_ref, bias_ref, tok, wg, wu, wd, ent, xbuf, part, ret, fin, sw, lsend, lrecv,
    in_sem, ent_ss, fr_ss, fl_ss, x_rs, rr_ss, rl_ss, ro_ss, r_rs, fx_ss, f_rs, l_ss, l_rs, hello,
):
    nxh, nz, nc = sizes
    width = tok.shape[1]
    xl, y = lax.axis_index("xl"), lax.axis_index("y")
    xh, z, c = lax.axis_index("xh"), lax.axis_index("z"), lax.axis_index("c")
    quad, s = lax.div(y, 4), lax.rem(y, 4)
    own = 2 * xl + quad
    mate = 1 - xl

    arrays = (
        (ids_hbm, ids_ref), (comb_hbm, comb_ref), (tok_hbm, tok), (wg_hbm, wg), (wu_hbm, wu),
        (wd_hbm, wd), (bias_hbm, bias_ref),
    )
    loads = [pltpu.make_async_copy(a, b, in_sem.at[k]) for k, (a, b) in enumerate(arrays)]
    for copy in loads:
        copy.start()

    nx = 2 * nxh
    xi = 2 * xh + xl
    y_peers = [(lax.rem(y + k, 8), {"y": lax.rem(y + k, 8)}) for k in range(1, 8)]
    x_peers = []
    for k in range(1, nx):
        other = lax.rem(xi + k, nx)
        x_peers.append((other, {"xl": lax.rem(other, 2), "xh": lax.div(other, 2)}))
    z_peers = [(lax.rem(z + k, nz), {"z": lax.rem(z + k, nz)}) for k in range(1, nz)]
    c_peers = [(lax.rem(c + k, nc), {"c": lax.rem(c + k, nc)}) for k in range(1, nc)]
    greeted = [where for _, where in y_peers] + [{"xl": mate}]
    for dy in (-2, -1, 1, 2):
        greeted.append({"xl": mate, "y": lax.rem(y + dy + 8, 8)})
    barrier = pltpu.get_barrier_semaphore()

    def signal(sem, where):
        pl.semaphore_signal(sem, inc=1, device_id=where, device_id_type=MESH)

    for where in greeted:
        signal(barrier, where)

    mate_at = 2 * xh + mate

    def x_asks(other):
        return (xi > other) & (other != mate_at)

    def x_answers(other):
        return (xi < other) & (other != mate_at)

    one_way = (
        (x_peers, x_asks, x_answers),
        (c_peers, lambda other: c > other, lambda other: c < other),
        (z_peers, lambda other: z < other, lambda other: z > other),
    )

    def count(peers, test):
        total = jnp.int32(0)
        for other, _ in peers:
            total = total + jnp.where(test(other), 1, 0)
        return total

    for peers, asks, _ in one_way:
        for other, where in peers:

            @pl.when(asks(other))
            def _():
                signal(barrier, where)

    loads[0].wait()
    loads[1].wait()
    ids = ids_ref[...]
    comb = comb_ref[...]
    row8 = lax.broadcasted_iota(jnp.int32, (8, 128), 0)
    exps = lax.broadcasted_iota(jnp.int32, (NEXP, 128), 0)
    hit = jnp.zeros((8, 128), f32)
    weight = jnp.zeros((8, 128), f32)
    many = jnp.zeros((NEXP, 128), f32)
    for p in range(TOPK):
        named = ids[p : p + 1, :]
        same = row8 == named
        hit += jnp.where(same, 1.0, 0.0)
        weight += jnp.where(same, comb[p : p + 1, :], 0.0)
        many += jnp.where(exps == named, 1.0, 0.0)
    before = lax.broadcasted_iota(jnp.int32, (128, 128), 0) < lax.broadcasted_iota(
        jnp.int32, (128, 128), 1
    )
    rank = jnp.dot(
        hit.astype(bf16), jnp.where(before, 1.0, 0.0).astype(bf16), preferred_element_type=f32
    )
    slots = lax.broadcasted_iota(jnp.int32, (CAP, 128), 0).astype(f32)
    select, scale = [], []
    for w in range(NWIN):
        there = jnp.where(slots == rank[w : w + 1, :], hit[w : w + 1, :], 0.0)
        select.append(there)
        scale.append(there * weight[w : w + 1, :])
    select = jnp.concatenate(select, axis=0).astype(bf16)
    scale = jnp.concatenate(scale, axis=0)
    high = scale.astype(bf16)
    rest = scale - high.astype(f32)
    middle = rest.astype(bf16)
    low = (rest - middle.astype(f32)).astype(bf16)
    sw[...] = jnp.concatenate([high, middle, low], axis=0)
    counts = lax.dot_general(
        jnp.ones((8, 128), bf16), many.astype(bf16), (((1,), (1,)), ((), ())),
        preferred_element_type=f32,
    )
    lsend[0] = counts

    loads[2].wait()
    step = width // PIECES
    for at in range(0, width, step):
        rows = jnp.dot(select, tok[:, at : at + step], preferred_element_type=f32)
        ent[:, at : at + step] = rows.astype(bf16)
    xbuf[s + 2, 0:CAP, :] = ent[pl.ds(pl.multiple_of(own * CAP, CAP), CAP), :]

    expected = jnp.int32(len(greeted))
    for peers, _, answers in one_way:
        expected = expected + count(peers, answers)
    pl.semaphore_wait(barrier, expected)
    for axis, (peers, _, answers) in enumerate(one_way):
        for other, where in peers:

            @pl.when(answers(other))
            def _():
                signal(hello.at[axis], where)


    entries = []
    for number, (k, dx) in enumerate(((0, 1), (1, 0), (1, 1))):
        tq = lax.rem(quad + k, 2)
        tx = lax.rem(xl + dx, 2)
        ry = lax.rem(y - 4 * tq + 8, 8)
        o = jnp.where(ry <= 5, ry, ry - 8)
        node = jnp.clip(o, 0, 3)
        w = 2 * tx + tq
        entries.append(
            pltpu.make_async_remote_copy(
                src_ref=ent.at[pl.ds(pl.multiple_of(w * CAP, CAP), CAP)],
                dst_ref=xbuf.at[o + 2, pl.ds(CAP * dx, CAP)],
                send_sem=ent_ss.at[number],
                recv_sem=x_rs.at[o + 2, dx],
                device_id={"xl": tx, "y": 4 * tq + node},
                device_id_type=MESH,
            )
        )

    def forward(i, xr, right):
        block = xbuf.at[i, pl.ds(CAP * xr, CAP)]
        return pltpu.make_async_remote_copy(
            src_ref=block,
            dst_ref=block,
            send_sem=(fr_ss if right else fl_ss).at[i],
            recv_sem=x_rs.at[i, xr],
            device_id={"y": lax.rem(y + (1 if right else 7), 8)},
            device_id_type=MESH,
        )

    entries[0].start()

    @pl.when(s < 2)
    def _():
        forward(s + 2, 0, True).start()

    @pl.when(s > 1)
    def _():
        forward(s + 2, 0, False).start()

    @pl.when((s == 1) | (s == 2))
    def _():
        entries[1].start()
        entries[2].start()

    def tell(phase, number, here, peers):
        made = []
        for k, (_, where) in enumerate(peers):
            made.append(
                pltpu.make_async_remote_copy(
                    src_ref=lsend.at[phase],
                    dst_ref=lrecv.at[phase, here],
                    send_sem=l_ss.at[phase],
                    recv_sem=l_rs.at[phase, here],
                    device_id=where,
                    device_id_type=MESH,
                )
            )
        return made

    phases = [(y, y_peers), (xi, x_peers), (c, c_peers), (z, z_peers)]

    def tell_all(phase):
        if phase > 0:
            peers, asks, _ = one_way[phase - 1]
            answers = count(peers, asks)

            @pl.when(answers > 0)
            def _():
                pl.semaphore_wait(hello.at[phase - 1], answers)

        for copy in tell(phase, None, phases[phase][0], phases[phase][1]):
            copy.start()

    def hear_all(phase):
        total = lsend[phase]
        for other, where in phases[phase][1]:
            pltpu.make_async_remote_copy(
                src_ref=lsend.at[phase],
                dst_ref=lrecv.at[phase, other],
                send_sem=l_ss.at[phase],
                recv_sem=l_rs.at[phase, other],
                device_id=where,
                device_id_type=MESH,
            ).wait_recv()
            total = total + lrecv[phase, other]
        return total

    tell_all(0)
    for copy in loads[3:]:
        copy.wait()

    def piece(ref, i, rows, q):
        return ref.at[i, rows, pl.ds(q * step, step)]

    both = pl.ds(0, 2 * CAP)

    def send_on(i, q, right):
        slot = i if right else jnp.where(i - 2 == s - 1, 8, i)
        return pltpu.make_async_remote_copy(
            src_ref=piece(ret, i, both, q),
            dst_ref=piece(ret, slot, both, q),
            send_sem=(rr_ss if right else rl_ss).at[i],
            recv_sem=r_rs.at[slot, q],
            device_id={"y": lax.rem(y + (1 if right else 7), 8)},
            device_id_type=MESH,
        )

    def send_out(i, q, xr):
        return pltpu.make_async_remote_copy(
            src_ref=piece(ret, i, pl.ds(CAP * xr, CAP), q),
            dst_ref=piece(fin, own, pl.ds(0, CAP), q),
            send_sem=ro_ss.at[i],
            recv_sem=f_rs.at[own, q],
            device_id={"xl": lax.rem(xl + xr, 2), "y": lax.rem(4 * quad + i + 6, 8)},
            device_id_type=MESH,
        )

    def arrived(i, q):
        block = piece(ret, i, both, q)
        pltpu.make_async_remote_copy(
            src_ref=block, dst_ref=block, send_sem=rr_ss.at[0], recv_sem=r_rs.at[i, q],
            device_id={"y": lax.rem(y + 1, 8)}, device_id_type=MESH,
        ).wait_recv()

    def to_mate(q):
        return pltpu.make_async_remote_copy(
            src_ref=piece(ret, 9, pl.ds(0, CAP), q),
            dst_ref=piece(fin, own, pl.ds(0, CAP), q),
            send_sem=fx_ss.at[0],
            recv_sem=f_rs.at[own, q],
            device_id={"xl": mate},
            device_id_type=MESH,
        )

    last = jnp.where((s == 0) | (s == 3), 6, 7)

    def line(k):
        return jnp.where(k <= 3, k, jnp.where(k == 6, 1, 9 - k))

    def round_(r, carry):
        ends = (s == 0) | (s == 3)
        both_in = ends & (r == 1)
        a_has = both_in | ((s == 3) & (r >= 2) & (r <= 6)) | ((r >= 1) & (r <= s + 2) & ~ends)
        b_has = both_in | ((s == 0) & (r >= 2) & (r <= 6)) | ((r >= 1) & (r <= 5 - s) & ~ends)
        a_in = jnp.where(r <= s, s - r, r - s - 3)
        b_in = jnp.where(r <= 3 - s, s + r, 9 - s - r)
        a_o = jnp.where(s == 0, -2, jnp.where(s == 3, jnp.where(r == 1, 5, 3 - line(r)), a_in))
        b_o = jnp.where(s == 3, 4, jnp.where(s == 0, jnp.where(r == 1, -1, line(r)), b_in))
        ia = jnp.where(a_has, a_o, s) + 2
        ib = jnp.where(b_has, b_o, s) + 2
        inner = (s == 1) | (s == 2)
        streams = (
            (ia, a_has, (inner & a_has) | ((s == 0) & (r == 1)), (s == 3) & (r == 1)),
            (ib, b_has, (s == 0) & (r == 1), (inner & b_has) | ((s == 3) & (r == 1))),
        )

        @pl.when(r == 0)
        def _():
            forward(s + 2, 1, True).wait_recv()

            @pl.when(s < 2)
            def _():
                forward(s + 2, 1, True).start()

            @pl.when(s > 1)
            def _():
                forward(s + 2, 1, False).start()

            @pl.when((s == 0) | (s == 3))
            def _():
                entries[1].start()
                entries[2].start()

        for i, has, go_right, go_left in streams:
            for xr in (0, 1):

                @pl.when(has)
                def _():
                    forward(i, xr, True).wait_recv()

                @pl.when(go_right)
                def _():
                    forward(i, xr, True).start()

                @pl.when(go_left)
                def _():
                    forward(i, xr, False).start()

        @pl.when((r == 4) & (s == 2))
        def _():
            forward(s + 2, 0, True).start()
            forward(s + 2, 1, True).start()

        @pl.when((r == 4) & (s == 1))
        def _():
            forward(s + 2, 0, False).start()
            forward(s + 2, 1, False).start()

        for phase, when in enumerate((2, 4, 5)):

            @pl.when(r == when)
            def _():
                lsend[phase + 1] = hear_all(phase)
                tell_all(phase + 1)

        @pl.when((r == 0) | a_has | b_has)
        def _():
            rows = jnp.concatenate([xbuf[ia], xbuf[ib]], axis=0)
            flat = (((1,), (1,)), ((), ()))
            gate = lax.dot_general(wg[...], rows, flat, preferred_element_type=f32)
            up = lax.dot_general(wu[...], rows, flat, preferred_element_type=f32)
            hidden = (jax.nn.silu(gate) * up).astype(bf16)
            for at in range(0, width, step):
                out = lax.dot_general(
                    hidden, wd[:, at : at + step], (((0,), (0,)), ((), ())),
                    preferred_element_type=f32,
                )
                part[ia, :, at : at + step] = out[: 2 * CAP]
                part[ib, :, at : at + step] = out[2 * CAP :]

        for q in range(PIECES):
            cols = slice(q * step, (q + 1) * step)
            for right in (True, False):
                at = s if right else 3 - s
                k = r - at
                along = line(k)
                valid = (k >= 2) & (k <= 6) & (along > at)
                o = along if right else 3 - along
                i = o + 2
                first = s == (0 if right else 3)
                end = s == (3 if right else 0)

                @pl.when(valid)
                def _():
                    @pl.when(first)
                    def _():
                        ret[i, :, cols] = part[i, :, cols].astype(bf16)

                    @pl.when(jnp.logical_not(first))
                    def _():
                        arrived(i, q)
                        ret[i, :, cols] = (part[i, :, cols] + ret[i, :, cols].astype(f32)).astype(
                            bf16
                        )

                    @pl.when(end)
                    def _():
                        send_out(i, q, 0).start()
                        send_out(i, q, 1).start()

                    @pl.when(jnp.logical_not(end))
                    def _():
                        send_on(i, q, right).start()

        @pl.when(r == last)
        def _():
            for q in range(PIECES):
                cols = slice(q * step, (q + 1) * step)

                @pl.when(s > 0)
                def _():
                    arrived(s + 2, q)
                    part[s + 2, :, cols] += ret[s + 2, :, cols].astype(f32)

                @pl.when(s < 3)
                def _():
                    arrived(8, q)
                    part[s + 2, :, cols] += ret[8, :, cols].astype(f32)

                ret[9, 0:CAP, cols] = part[s + 2, CAP : 2 * CAP, cols].astype(bf16)
                to_mate(q).start()
                fin[own, :, cols] = part[s + 2, 0:CAP, cols].astype(bf16)

        return carry

    lax.fori_loop(0, 9, round_, 0)

    def drained(ref, i, sem, rows=2 * CAP):
        block = ref.at[i, pl.ds(0, rows)]
        pltpu.make_async_remote_copy(
            src_ref=block, dst_ref=block, send_sem=sem, recv_sem=f_rs.at[0, 0],
            device_id={"xl": mate}, device_id_type=MESH,
        ).wait_send()

    for copy in entries:
        copy.wait_send()
    for phase in range(4):
        told = len(phases[phase][1])
        if told:
            drained(lrecv, phase, l_ss.at[phase], told)

    def drain_rows(i, carry):
        @pl.when((s < 3) & (i - 2 <= s))
        def _():
            drained(xbuf, i, fr_ss.at[i])

        @pl.when((s > 0) & (i - 2 >= s))
        def _():
            drained(xbuf, i, fl_ss.at[i])

        return carry

    lax.fori_loop(0, 8, drain_rows, 0)

    load = hear_all(3)[0:1, :]
    nb_ref[...] = bias_ref[...] - 0.05 * (load - mean_load) / math.sqrt(mean_load)
    for q in range(PIECES):
        cols = slice(q * step, (q + 1) * step)
        for k, dx in ((0, 1), (1, 0), (1, 1)):
            w = 2 * lax.rem(xl + dx, 2) + lax.rem(quad + k, 2)
            pltpu.make_async_remote_copy(
                src_ref=piece(ret, 9, pl.ds(0, CAP), q),
                dst_ref=piece(fin, w, pl.ds(0, CAP), q),
                send_sem=fx_ss.at[0],
                recv_sem=f_rs.at[w, q],
                device_id={"xl": mate},
                device_id_type=MESH,
            ).wait_recv()
        done = fin[:, :, cols].reshape(NWIN * CAP, step)
        done = jnp.concatenate([done, done, done], axis=0)
        mixed_ref[:, cols] = lax.dot_general(
            sw[...], done, (((0,), (0,)), ((), ())), preferred_element_type=f32
        ).astype(bf16)

    drained(ret, 9, fx_ss.at[0], CAP)

    def drain(i, carry):
        o = i - 2

        @pl.when((o > s) & (s < 3))
        def _():
            drained(ret, i, rr_ss.at[i])

        @pl.when((o < s) & (s > 0))
        def _():
            drained(ret, i, rl_ss.at[i])

        @pl.when(((s == 3) & (o > 3)) | ((s == 0) & (o < 0)))
        def _():
            drained(ret, i, ro_ss.at[i])

        return carry

    lax.fori_loop(0, 8, drain, 0)


def per_device(sizes, tokens, expert_ids, combine, w_gate, w_up, w_down, bias):
    tok_rows, width = tokens.shape
    hidden = w_down.shape[0]
    devices = 16 * math.prod(sizes)
    mean_load = float(tok_rows * devices * TOPK / NEXP)
    vmem = pl.BlockSpec(memory_space=pltpu.VMEM)
    hbm = pl.BlockSpec(memory_space=pl.ANY)
    dma = pltpu.SemaphoreType.DMA
    mixed, new_bias = pl.pallas_call(
        functools.partial(kernel, sizes, mean_load),
        out_shape=(
            jax.ShapeDtypeStruct((tok_rows, width), bf16),
            jax.ShapeDtypeStruct((1, NEXP), f32),
        ),
        in_specs=[hbm] * 7,
        out_specs=(vmem, vmem),
        scratch_shapes=[
            pltpu.VMEM((TOPK, tok_rows), jnp.int32),
            pltpu.VMEM((TOPK, tok_rows), f32),
            pltpu.VMEM((1, NEXP), f32),
            pltpu.VMEM((tok_rows, width), bf16),
            pltpu.VMEM((hidden, width), bf16),
            pltpu.VMEM((hidden, width), bf16),
            pltpu.VMEM((hidden, width), bf16),
            pltpu.VMEM((NWIN * CAP, width), bf16),
            pltpu.VMEM((8, 2 * CAP, width), bf16),
            pltpu.VMEM((8, 2 * CAP, width), f32),
            pltpu.VMEM((10, 2 * CAP, width), bf16),
            pltpu.VMEM((NWIN, CAP, width), bf16),
            pltpu.VMEM((3 * NWIN * CAP, 128), bf16),
            pltpu.VMEM((4, 8, 128), f32),
            pltpu.VMEM((4, 8, 8, 128), f32),
            dma((7,)),
            dma((3,)),
            dma((8,)),
            dma((8,)),
            dma((8, 2)),
            dma((8,)),
            dma((8,)),
            dma((8,)),
            dma((10, PIECES)),
            dma((1,)),
            dma((NWIN, PIECES)),
            dma((4,)),
            dma((4, 8)),
            pltpu.SemaphoreType.REGULAR((3,)),
        ],
        compiler_params=pltpu.CompilerParams(
            collective_id=0, has_side_effects=True, vmem_limit_bytes=67043328
        ),
        name="moe",
    )(
        expert_ids.T, combine.T, bias.reshape(1, NEXP), tokens, w_gate.T, w_up.T, w_down,
    )
    return mixed, new_bias.reshape(NEXP)


def solution(mesh):
    devices = mesh.devices
    ep, grp = devices.shape
    shape = (2, 8, 4, 8, 2) if (ep, grp) == (16, 64) else (2, 8, 1, 1, grp)
    finer = Mesh(devices.reshape(shape), AXES)
    row = P(AXES, None)
    in_specs = (row, row, row, P(None, ("xl", "y")), P(None, ("xl", "y")), P(("xl", "y"), None), P())
    return jax.shard_map(
        functools.partial(per_device, shape[2:]), mesh=finer, in_specs=in_specs,
        out_specs=(row, P()), check_vma=False,
    )
```

time: 100 us -> 80 us (0.80)
  the two profiles are of different devices: /device:TPU:36 before, /device:TPU:2 now
where the time goes in v2:
time: 80 us; the launch traced here: 79.8 us
  Pallas kernels  75.8 us (95%)
  local copies, waits for them, and re-layouts  3.4 us (4%)
    pallas_call x1, Pallas kernels, per_device(): pl.pallas_call(functools.partial(kernel, sizes, mean_load), out_shape=(ja...  75.8 us
    unnamed x2, local copies, waits for them, and re-layouts  3.4 us

profile of v2, /device:TPU:2, one launch (start us, length us, event | category | flops | bytes accessed | tf_op | source)
XLA Modules:
  0.0 79.8 jit_solution(15199441551692692442)
XLA Ops:
  0.6 75.8 %moe.1 = (bf16[128,4096]{1,0:T(8,128)(2,1)}, f32[1,128]{1,0:T(1,128)}) custom-call(s32[8,128]{1,0:T(8,128)} %bitcast.8, f32[8,128]{1,0:T(8,128)} %bitcast.9, f32[1,128]{1,0:T(1,128)} %bitcast.10, bf16[128,4096]{1,0:T(8,128)(2,1)} %tok_hbm.1, bf16[320,4096]{1,0:T(8,128)(2,1)} %bitcast.6, bf16[320,4096]{1,0:T(8,128)(2,1)} %bitcast.7, bf16[320,4096]{1,0:T(8,128)(2,1)} %wd_hbm.1), custom_call_target="tpu_custom_call" | custom-call | tf_op jit(solution)/shard_map/moe/pallas_call | solution.py:507
  76.4 2.3 %copy.11 = bf16[128,4096]{1,0:T(8,128)(2,1)} copy(bf16[128,4096]{1,0:T(8,128)(2,1)} %get-tuple-element.8) | data formatting | bytes 2097152
  78.7 1.1 %copy.12 = f32[128]{0:T(128)} copy(f32[128]{0:T(128)} %bitcast.11) | data formatting | bytes 1024

commit v3 on v2

--- a/solution.py
+++ b/solution.py
@@ -21,11 +21,11 @@
 
 
 def kernel(
-    sizes, mean_load,
-    ids_hbm, comb_hbm, bias_hbm, tok_hbm, wg_hbm, wu_hbm, wd_hbm,
-    mixed_ref, nb_ref,
-    ids_ref, comb_ref, bias_ref, tok, wg, wu, wd, ent, xbuf, part, ret, fin, sw, lsend, lrecv,
-    in_sem, ent_ss, fr_ss, fl_ss, x_rs, rr_ss, rl_ss, ro_ss, r_rs, fx_ss, f_rs, l_ss, l_rs, hello,
+    sizes,
+    ids_hbm, comb_hbm, tok_hbm, wg_hbm, wu_hbm, wd_hbm,
+    fin_hbm, sw_hbm, load_hbm,
+    ids_ref, comb_ref, load_ref, tok, wg, wu, wd, ent, xbuf, part, ret, fin, sw, lsend, lrecv,
+    in_sem, ent_ss, fr_ss, fl_ss, x_rs, rr_ss, rl_ss, ro_ss, r_rs, fx_ss, f_rs, l_ss, l_rs, hello, out_sem,
 ):
     nxh, nz, nc = sizes
     width = tok.shape[1]
@@ -37,7 +37,7 @@
 
     arrays = (
         (ids_hbm, ids_ref), (comb_hbm, comb_ref), (tok_hbm, tok), (wg_hbm, wg), (wu_hbm, wu),
-        (wd_hbm, wd), (bias_hbm, bias_ref),
+        (wd_hbm, wd),
     )
     loads = [pltpu.make_async_copy(a, b, in_sem.at[k]) for k, (a, b) in enumerate(arrays)]
     for copy in loads:
@@ -124,6 +124,8 @@
     middle = rest.astype(bf16)
     low = (rest - middle.astype(f32)).astype(bf16)
     sw[...] = jnp.concatenate([high, middle, low], axis=0)
+    sw_out = pltpu.make_async_copy(sw, sw_hbm, out_sem.at[0])
+    load_out = pltpu.make_async_copy(load_ref, load_hbm, out_sem.at[1])
     counts = lax.dot_general(
         jnp.ones((8, 128), bf16), many.astype(bf16), (((1,), (1,)), ((), ())),
         preferred_element_type=f32,
@@ -370,20 +372,20 @@
                 part[ia, :, at : at + step] = out[: 2 * CAP]
                 part[ib, :, at : at + step] = out[2 * CAP :]
 
-        for q in range(PIECES):
-            cols = slice(q * step, (q + 1) * step)
-            for right in (True, False):
-                at = s if right else 3 - s
-                k = r - at
-                along = line(k)
-                valid = (k >= 2) & (k <= 6) & (along > at)
-                o = along if right else 3 - along
-                i = o + 2
-                first = s == (0 if right else 3)
-                end = s == (3 if right else 0)
-
-                @pl.when(valid)
-                def _():
+        def sums(right, turn):
+            at = s if right else 3 - s
+            k = r - at
+            along = line(k)
+            valid = (k >= 2) & (k <= 6) & (along > at) & turn
+            i = (along if right else 3 - along) + 2
+            first = s == (0 if right else 3)
+            end = s == (3 if right else 0)
+
+            @pl.when(valid)
+            def _():
+                for q in range(PIECES):
+                    cols = slice(q * step, (q + 1) * step)
+
                     @pl.when(first)
                     def _():
                         ret[i, :, cols] = part[i, :, cols].astype(bf16)
@@ -404,6 +406,10 @@
                     def _():
                         send_on(i, q, right).start()
 
+        sums(False, s >= 2)
+        sums(True, s >= 0)
+        sums(False, s < 2)
+
         @pl.when(r == last)
         def _():
             for q in range(PIECES):
@@ -454,10 +460,15 @@
 
     lax.fori_loop(0, 8, drain_rows, 0)
 
-    load = hear_all(3)[0:1, :]
-    nb_ref[...] = bias_ref[...] - 0.05 * (load - mean_load) / math.sqrt(mean_load)
+    sw_out.start()
+    load_ref[...] = hear_all(3)
+    load_out.start()
+
+    def fin_out(q):
+        cols = pl.ds(q * step, step)
+        return pltpu.make_async_copy(fin.at[:, :, cols], fin_hbm.at[:, :, cols], out_sem.at[2 + q])
+
     for q in range(PIECES):
-        cols = slice(q * step, (q + 1) * step)
         for k, dx in ((0, 1), (1, 0), (1, 1)):
             w = 2 * lax.rem(xl + dx, 2) + lax.rem(quad + k, 2)
             pltpu.make_async_remote_copy(
@@ -468,11 +479,7 @@
                 device_id={"xl": mate},
                 device_id_type=MESH,
             ).wait_recv()
-        done = fin[:, :, cols].reshape(NWIN * CAP, step)
-        done = jnp.concatenate([done, done, done], axis=0)
-        mixed_ref[:, cols] = lax.dot_general(
-            sw[...], done, (((0,), (0,)), ((), ())), preferred_element_type=f32
-        ).astype(bf16)
+        fin_out(q).start()
 
     drained(ret, 9, fx_ss.at[0], CAP)
 
@@ -494,6 +501,31 @@
         return carry
 
     lax.fori_loop(0, 8, drain, 0)
+    sw_out.wait()
+    load_out.wait()
+    for q in range(PIECES):
+        fin_out(q).wait()
+
+
+def finish(mean_load, fin_ref, sw_ref, load_ref, bias_ref, mixed_hbm, nb_ref, out, out_sem):
+    width = out.shape[1]
+    step = width // PIECES
+    copies = []
+    for q in range(PIECES):
+        cols = slice(q * step, (q + 1) * step)
+        done = fin_ref[:, :, cols].reshape(NWIN * CAP, step)
+        done = jnp.concatenate([done, done, done], axis=0)
+        out[:, cols] = lax.dot_general(
+            sw_ref[...], done, (((0,), (0,)), ((), ())), preferred_element_type=f32
+        ).astype(bf16)
+        span = pl.ds(q * step, step)
+        copies.append(
+            pltpu.make_async_copy(out.at[:, span], mixed_hbm.at[:, span], out_sem.at[q])
+        )
+        copies[-1].start()
+    nb_ref[...] = bias_ref[...] - 0.05 * (load_ref[0:1, :] - mean_load) / math.sqrt(mean_load)
+    for copy in copies:
+        copy.wait()
 
 
 def per_device(sizes, tokens, expert_ids, combine, w_gate, w_up, w_down, bias):
@@ -501,21 +533,21 @@
     hidden = w_down.shape[0]
     devices = 16 * math.prod(sizes)
     mean_load = float(tok_rows * devices * TOPK / NEXP)
-    vmem = pl.BlockSpec(memory_space=pltpu.VMEM)
     hbm = pl.BlockSpec(memory_space=pl.ANY)
     dma = pltpu.SemaphoreType.DMA
-    mixed, new_bias = pl.pallas_call(
-        functools.partial(kernel, sizes, mean_load),
+    fin, sw, load = pl.pallas_call(
+        functools.partial(kernel, sizes),
         out_shape=(
-            jax.ShapeDtypeStruct((tok_rows, width), bf16),
-            jax.ShapeDtypeStruct((1, NEXP), f32),
+            jax.ShapeDtypeStruct((NWIN, CAP, width), bf16),
+            jax.ShapeDtypeStruct((3 * NWIN * CAP, tok_rows), bf16),
+            jax.ShapeDtypeStruct((8, NEXP), f32),
         ),
-        in_specs=[hbm] * 7,
-        out_specs=(vmem, vmem),
+        in_specs=[hbm] * 6,
+        out_specs=(hbm, hbm, hbm),
         scratch_shapes=[
             pltpu.VMEM((TOPK, tok_rows), jnp.int32),
             pltpu.VMEM((TOPK, tok_rows), f32),
-            pltpu.VMEM((1, NEXP), f32),
+            pltpu.VMEM((8, NEXP), f32),
             pltpu.VMEM((tok_rows, width), bf16),
             pltpu.VMEM((hidden, width), bf16),
             pltpu.VMEM((hidden, width), bf16),
@@ -528,7 +560,7 @@
             pltpu.VMEM((3 * NWIN * CAP, 128), bf16),
             pltpu.VMEM((4, 8, 128), f32),
             pltpu.VMEM((4, 8, 8, 128), f32),
-            dma((7,)),
+            dma((6,)),
             dma((3,)),
             dma((8,)),
             dma((8,)),
@@ -542,14 +574,27 @@
             dma((4,)),
             dma((4, 8)),
             pltpu.SemaphoreType.REGULAR((3,)),
+            dma((2 + PIECES,)),
         ],
         compiler_params=pltpu.CompilerParams(
             collective_id=0, has_side_effects=True, vmem_limit_bytes=67043328
         ),
         name="moe",
     )(
-        expert_ids.T, combine.T, bias.reshape(1, NEXP), tokens, w_gate.T, w_up.T, w_down,
+        expert_ids.T, combine.T, tokens, w_gate.T, w_up.T, w_down,
     )
+    vmem = pl.BlockSpec(memory_space=pltpu.VMEM)
+    mixed, new_bias = pl.pallas_call(
+        functools.partial(finish, mean_load),
+        out_shape=(
+            jax.ShapeDtypeStruct((tok_rows, width), bf16),
+            jax.ShapeDtypeStruct((1, NEXP), f32),
+        ),
+        in_specs=[vmem] * 4,
+        out_specs=(hbm, vmem),
+        scratch_shapes=[pltpu.VMEM((tok_rows, width), bf16), dma((PIECES,))],
+        name="finish",
+    )(fin, sw, load, bias.reshape(1, NEXP))
     return mixed, new_bias.reshape(NEXP)
 
 

time: 80 us -> 78.4 us (0.980)
  local copies, waits for them, and re-layouts: 3.4 us -> 0 us
  Pallas kernels: 75.8 us -> 77.6 us
    unnamed x2 -> x0, local copies, waits for them, and re-layouts: 3.4 us -> none
    pallas_call x1 -> x2, Pallas kernels: 75.8 us -> 77.6 us  [the longest x1 74.7 us: per_device(): pl.pallas_call(functools.partial(kernel, sizes), out_shape=(jax.ShapeDtyp...]
where the time goes in v3:
time: 78.4 us; the launch traced here: 78.2 us
  Pallas kernels  77.6 us (99%)
    pallas_call x1, Pallas kernels, per_device(): pl.pallas_call(functools.partial(kernel, sizes), out_shape=(jax.ShapeDtyp...  74.7 us
    pallas_call x1, Pallas kernels, per_device(): pl.pallas_call(functools.partial(finish, mean_load), out_shape=(jax.Shape...  2.84 us

profile of v3, /device:TPU:2, one launch (start us, length us, event | category | flops | bytes accessed | tf_op | source)
XLA Modules:
  0.0 78.2 jit_solution(6594747549351409187)
XLA Ops:
  0.6 74.7 %moe.1 = (bf16[4,16,4096]{2,1,0:T(8,128)(2,1)}, bf16[192,128]{1,0:T(8,128)(2,1)}, f32[8,128]{1,0:T(8,128)}) custom-call(s32[8,128]{1,0:T(8,128)} %bitcast.8, f32[8,128]{1,0:T(8,128)} %bitcast.9, bf16[128,4096]{1,0:T(8,128)(2,1)} %tok_hbm.1, bf16[320,4096]{1,0:T(8,128)(2,1)} %bitcast.6, bf16[320,4096]{1,0:T(8,128)(2,1)} %bitcast.7, bf16[320,4096]{1,0:T(8,128)(2,1)} %wd_hbm.1), custom_call_target="tpu_custom_call" | custom-call | tf_op jit(solution)/shard_map/moe/pallas_call | solution.py:538
  75.4 2.8 %finish.1 = (bf16[128,4096]{1,0:T(8,128)(2,1)}, f32[1,128]{1,0:T(1,128)}) custom-call(bf16[4,16,4096]{2,1,0:T(8,128)(2,1)} %get-tuple-element.7.fin_ref, bf16[192,128]{1,0:T(8,128)(2,1)} %get-tuple-element.8.sw_ref, f32[8,128]{1,0:T(8,128)} %get-tuple-element.9.load_ref, f32[1,128]{1,0:T(1,128)} %bitcast.10), custom_call_target="tpu_custom_call" | custom-call | tf_op jit(solution)/shard_map/finish/pallas_call | solution.py:587
